TPU v7x, 512 devices: a whole 4x8x8 slice. The times are simulated.
512 devices in a mesh: dp: 8 (over x, core), vocab: 64 (over y, z).
Axes of the slice: x: 4, y: 8, z: 8, core: 2. Of those that a mesh axis runs over, the one named last changes fastest.
Arguments:
- hidden: bfloat16 [1792, 4608], P('dp'), may hold values from -15 to 15
- out_weight: bfloat16 [4608, 24576], P('dp', 'vocab'), may hold values from -0.09375 to 0.09375
- targets: int32 [1792], P('dp'), may hold values from 0 to 24383
- token_weight: float32 [1792], P('dp'), may hold values from 0.3 to 3
Outputs:
- token_loss: float32 [1792], P('dp')
- hidden_grad: bfloat16 [1792, 4608], P('dp')
- weight_grad: bfloat16 [4608, 24576], P('dp', 'vocab')
All inputs are finite; a program needn't handle non-finite values.
Results may differ from a plain program's by a relative error of at most 0.0085.
Values may be sent and summed in bfloat16 or wider, within the bound.
A program may use at most 64 MiB of HBM per device.

v0:
```python
import jax
import jax.numpy as jnp
from jax import lax
from jax.sharding import Mesh
from jax.sharding import PartitionSpec as P

VOCAB = ("vocab_0", "vocab_1")


softcap = 30.0


def by_axis(array, axes):
    for axis in axes:
        array = lax.psum(array, axis)
    return array


def in_blocks(array, dim, peers):
    before, after = (array.shape[:dim], array.shape[dim + 1 :])
    return jnp.moveaxis(array.reshape(*before, peers, -1, *after), dim, 0)


def sent_and_summed(array, axis, dim):
    blocks = in_blocks(array, dim, lax.axis_size(axis))
    arrived = lax.all_to_all(blocks, axis, split_axis=0, concat_axis=0, tiled=True)
    return arrived.astype(jnp.float32).sum(axis=0)


def from_everyone(array, axis):
    peers = lax.axis_size(axis)
    return lax.all_to_all(
        jnp.broadcast_to(array[None], (peers, *array.shape)), axis, 0, 0, tiled=True
    )


def in_order(blocks, dim):
    blocks = jnp.moveaxis(blocks, 0, dim)
    lengths = blocks.shape
    return blocks.reshape(*lengths[:dim], lengths[dim] * lengths[dim + 1], *lengths[dim + 2 :])


def gather_directly(array, axis, dim):
    blocks = from_everyone(array, axis)
    return in_order(blocks, dim)


def body(hidden, out_weight, targets, token_weight):
    shard_width = out_weight.shape[1]
    row_count = out_weight.shape[0]
    tok_rows = hidden.shape[0]
    vocab_used = shard_width * lax.axis_size(VOCAB) - shard_width // 2
    first_col = lax.axis_index(VOCAB) * shard_width
    col_ids = first_col + jnp.arange(shard_width, dtype=jnp.int32)
    usable = col_ids < vocab_used
    w_full = lax.all_gather(out_weight, "dp", axis=0, tiled=True)
    logits = jnp.dot(hidden, w_full, preferred_element_type=jnp.float32)
    squash = jnp.tanh(logits / softcap)
    capped = softcap * squash
    exp_terms = jnp.where(usable[None, :], jnp.exp(capped), jnp.float32(0.0))
    target_hit = col_ids[None, :] == targets[:, None]
    local_sum = jnp.sum(exp_terms, axis=1)
    local_target = jnp.sum(jnp.where(target_hit, capped, jnp.float32(0.0)), axis=1)
    sums, target_logit = (by_axis(local_sum, VOCAB), by_axis(local_target, VOCAB))
    token_loss = jnp.log(sums) - target_logit
    onehot = jnp.where(target_hit, jnp.float32(1.0), jnp.float32(0.0))
    logit_grad = (
        token_weight[:, None] * (exp_terms / sums[:, None] - onehot) * (1.0 - squash * squash)
    ).astype(jnp.bfloat16)
    contract_cols = (((1,), (1,)), ((), ()))
    partial_grad = lax.dot_general(
        logit_grad, w_full, contract_cols, preferred_element_type=jnp.float32
    )
    share = sent_and_summed(partial_grad.astype(jnp.bfloat16), VOCAB, 1).astype(jnp.bfloat16)
    hidden_grad = lax.all_gather(share, VOCAB, axis=1, tiled=True)
    owned_cols = lax.all_to_all(hidden, "dp", split_axis=1, concat_axis=0, tiled=True)
    every_grad = gather_directly(logit_grad, "dp", 0)
    block_count = owned_cols.shape[0] // tok_rows
    col_blocks = owned_cols.reshape(block_count, tok_rows, row_count)
    grad_blocks = every_grad.reshape(block_count, tok_rows, shard_width)
    block_terms = jnp.einsum(
        "ntr,ntv->nrv", col_blocks, grad_blocks, preferred_element_type=jnp.float32
    ).astype(jnp.bfloat16)
    weight_grad = jnp.sum(block_terms.astype(jnp.float32), axis=0).astype(jnp.bfloat16)
    return (token_loss, hidden_grad, weight_grad)


def solution(mesh):
    torus = Mesh(mesh.devices.reshape(mesh.shape["dp"], 8, 8), ("dp", "vocab_0", "vocab_1"))
    in_specs = (P("dp", None), P("dp", VOCAB), P("dp"), P("dp"))
    out_specs = (P("dp"), P("dp", None), P("dp", VOCAB))
    return jax.shard_map(body, mesh=torus, in_specs=in_specs, out_specs=out_specs, check_vma=False)
```

profile of v0, /device:TPU:1, one launch (start us, length us, event | category | flops | bytes accessed | tf_op | source)
XLA Modules:
  0.0 240.9 jit_solution(11273807396610826851)
XLA Ops:
  7.2 0.0 all-gather.3.cloned.1.call-start
  7.2 0.7 all-gather.3.cloned.1.call-update
  7.9 0.0 all-gather.5.cloned.1.call-start
  8.0 0.0 copy-start
  8.0 0.0 copy-start.1
  8.0 42.6 %all-gather.3.cloned.1.call-done = bf16[4608,384]{1,0:T(8,128)(2,1)} async-done(((bf16[576,384]{1,0:T(8,128)(2,1)}), bf16[4608,384]{1,0:T(8,128)(2,1)}) %all-gather.3.cloned.1.call-update) | async-done | bytes 3538960 | tf_op jit(solution)/shard_map/all_gather | solution.py:56
  50.6 4.1 %fusion.7 = (f32[224]{0:T(256)S(1)}, f32[224]{0:T(256)S(1)}, f32[224,384]{1,0:T(8,128)S(1)}) fusion(pred[384]{0:T(512)(128)(4,1)S(1)} %broadcast_compare_fusion, s32[224]{0:T(256)} %param.6, s32[384]{0:T(512)S(1)} %iota_add_fusion, bf16[224,4608]{1,0:T(8,128)(2,1)} %param.4, bf16[4608,384]{1,0:T(8,128)(2,1)} %all-gather.3.cloned.1.call-done), kind=kOutput, calls=%fused_computation.13 | convolution fusion | flops 793325056 | bytes 5952000 | tf_op jit(solution)/shard_map/dot_general | solution.py:57
  54.7 13.5 %all-reduce.1 = (f32[224]{0:T(256)S(1)}, f32[224]{0:T(256)S(1)}) all-reduce(f32[224]{0:T(256)S(1)} %get-tuple-element.7, f32[224]{0:T(256)S(1)} %get-tuple-element.6), channel_id=1, replica_groups=mesh['dp'=8,'vocab_0'=8,'vocab_1'=8] {'vocab_0'}, use_global_device_ids=true, to_apply=%region_4.5 | all-reduce | flops 448 | bytes 3584 | tf_op jit(solution)/shard_map/psum | solution.py:15
  68.2 14.3 %all-reduce = (f32[224]{0:T(256)S(1)}, f32[224]{0:T(256)S(1)}) all-reduce(f32[224]{0:T(256)S(1)} %get-tuple-element.10, f32[224]{0:T(256)S(1)} %get-tuple-element.11), channel_id=1, replica_groups=mesh['dp'=8,'vocab_0'=8,'vocab_1'=8] {'vocab_1'}, use_global_device_ids=true, to_apply=%region_5.6 | all-reduce | flops 448 | bytes 3584 | tf_op jit(solution)/shard_map/psum | solution.py:15
  82.5 0.0 copy-done
  82.5 0.0 copy-done.1
  82.5 0.2 fusion.6
  82.7 3.4 %convolution_convert_fusion = bf16[224,4608]{1,0:T(8,128)(2,1)S(1)} fusion(bf16[224,384]{1,0:T(8,128)(2,1)S(1)} %fusion.6, bf16[4608,384]{1,0:T(8,128)(2,1)} %all-gather.3.cloned.1.call-done), kind=kOutput, calls=%fused_computation | convolution fusion | flops 793755648 | bytes 5775360 | tf_op jit(solution)/shard_map/dot_general | solution.py:71
  86.1 2.4 %copy.9 = bf16[224,4608]{0,1:T(8,128)(2,1)} copy(bf16[224,4608]{1,0:T(8,128)(2,1)S(1)} %convolution_convert_fusion) | data formatting | bytes 4128768 | tf_op jit(solution)/shard_map/convert_element_type | solution.py:74
  88.6 59.4 %all_to_all.26 = bf16[64,224,72]{1,2,0:T(8,128)(2,1)S(1)} all-to-all(bf16[64,224,72]{1,2,0:T(8,128)(2,1)} %bitcast.12), channel_id=1, replica_groups=mesh['dp'=8,'vocab_0'=8,'vocab_1'=8] {'vocab_0','vocab_1'}, dimensions={0} | all-to-all | bytes 4128768 | tf_op jit(solution)/shard_map/all_to_all | solution.py:26
  147.9 1.0 reduce_sum.46
  149.0 0.0 all-gather.5.cloned.1.call-update
  149.0 3.6 %all_to_all.20 = bf16[224,8,576]{2,1,0:T(8,128)(2,1)S(1)} reshape(bf16[224,4608]{1,0:T(8,128)(2,1)} %param.4) | data formatting | bytes 4128768 | tf_op jit(solution)/shard_map/all_to_all | solution.py:76
  152.6 0.3 copy.10
  152.8 40.1 %all_to_all.27 = bf16[224,8,576]{2,0,1:T(8,128)(2,1)S(1)} all-to-all(bf16[224,8,576]{2,0,1:T(8,128)(2,1)S(1)} %copy.10), channel_id=1, replica_groups=mesh['dp'=8,'vocab_0'=8,'vocab_1'=8] {'dp'}, dimensions={1} | all-to-all | bytes 4128768 | tf_op jit(solution)/shard_map/all_to_all | solution.py:76
  193.0 1.2 broadcast_in_dim.34
  194.2 5.0 %all-to-all-start.1 = ((bf16[8,224,384]{2,1,0:T(8,128)(2,1)}), bf16[8,224,384]{2,1,0:T(8,128)(2,1)}, u32[]{:S(2)}, u32[]{:S(2)}) async-start(bf16[8,224,384]{2,1,0:T(8,128)(2,1)} %broadcast_in_dim.34), calls=%async_computation.1 | async-start | bytes 2752512 | tf_op jit(solution)/shard_map/all_to_all | solution.py:32
  199.2 0.6 log_subtract_fusion
  199.8 18.0 %all-to-all-done.1 = bf16[8,224,384]{2,1,0:T(8,128)(2,1)} async-done(((bf16[8,224,384]{2,1,0:T(8,128)(2,1)}), bf16[8,224,384]{2,1,0:T(8,128)(2,1)}, u32[]{:S(2)}, u32[]{:S(2)}) %all-to-all-start.1) | async-done | bytes 1376288 | tf_op jit(solution)/shard_map/all_to_all | solution.py:32
  217.8 3.6 %convert_reduce_fusion = bf16[384,576]{0,1:T(8,128)(2,1)} fusion(bf16[8,224,384]{2,1,0:T(8,128)(2,1)} %all-to-all-done.1, bf16[224,8,576]{2,0,1:T(8,128)(2,1)S(1)} %all_to_all.27), kind=kOutput, calls=%fused_computation.1 | convolution fusion | flops 796041216 | bytes 3883008 | tf_op jit(solution)/shard_map/ntr,ntv->nrv/dot_general | solution.py:81
  221.5 8.4 %all-gather.5.cloned.1.call-done = bf16[224,4608]{0,1:T(8,128)(2,1)} async-done(((bf16[224,72]{0,1:T(8,128)(2,1)}), bf16[224,4608]{0,1:T(8,128)(2,1)}) %all-gather.5.cloned.1.call-update) | async-done | bytes 2064400 | tf_op jit(solution)/shard_map/all_gather | solution.py:75
  229.9 4.1 %copy.11 = bf16[224,4608]{1,0:T(8,128)(2,1)} copy(bf16[224,4608]{0,1:T(8,128)(2,1)} %all-gather.5.cloned.1.call-done) | data formatting | bytes 4128768
  (2 shorter events, 0.0 us)
Async XLA Ops:
  7.2 43.5 %all-gather.3.cloned.1.call-start = ((), (), s32[]{:S(2)}) async-start(), calls=%async_computation.3 | async-start | bytes 3981312 | tf_op jit(solution)/shard_map/all_gather | solution.py:56
  7.9 222.0 %all-gather.5.cloned.1.call-start = ((), (), s32[]{:S(2)}) async-start(), calls=%async_computation.4 | async-start | bytes 2396160 | tf_op jit(solution)/shard_map/all_gather | solution.py:75
  8.0 74.6 %copy-start = (s32[224]{0:T(256)S(1)}, s32[224]{0:T(256)}, u32[]{:S(2)}) copy-start(s32[224]{0:T(256)} %param.6) | copy-start | bytes 2692
  8.0 74.6 %copy-start.1 = (f32[224]{0:T(256)S(1)}, f32[224]{0:T(256)}, u32[]{:S(2)}) copy-start(f32[224]{0:T(256)} %param.7) | copy-start | bytes 2692
  194.2 23.7 %all-to-all-start.1 = ((bf16[8,224,384]{2,1,0:T(8,128)(2,1)}), bf16[8,224,384]{2,1,0:T(8,128)(2,1)}, u32[]{:S(2)}, u32[]{:S(2)}) async-start(bf16[8,224,384]{2,1,0:T(8,128)(2,1)} %broadcast_in_dim.34), calls=%async_computation.1 | async-start | bytes 2752512 | tf_op jit(solution)/shard_map/all_to_all | solution.py:32
Sparse Core Ops, SparseCore 0:
  10.1 40.5 all-gather.2
  149.1 80.7 all-gather.4
where the time goes:
time: 244 us; the launch traced here: 241 us
  blocking collectives  127 us (52%)
  waiting for transfers between devices  69.8 us (29%)
  between operations  14.1 us (6%)
  local copies, waits for them, and re-layouts  11.6 us (5%)
  matrix products  11.1 us (5%)
  starting transfers between devices  5.12 us (2%)
    all_to_all x1, blocking collectives, sent_and_summed(): lax.all_to_all(blocks, axis, split_axis=0, concat_axis=0, tiled=True)  59.4 us
    all_gather x1, waiting for transfers between devices, body(): w_full = lax.all_gather(out_weight, 'dp', axis=0, tiled=True)  42.6 us
    all_to_all x1, blocking collectives, body(): lax.all_to_all(hidden, 'dp', split_axis=1, concat_axis=0, tiled=True)  40.1 us
    psum x2, blocking collectives, by_axis(): array = lax.psum(array, axis)  27.8 us
    all_to_all x1, waiting for transfers between devices, from_everyone(): lax.all_to_all(jnp.broadcast_to(array[None], (peers, *array.shape)), axis...  18 us
    all_gather x1, waiting for transfers between devices, body(): hidden_grad = lax.all_gather(share, VOCAB, axis=1, tiled=True)  8.43 us
    all_to_all x1, starting transfers between devices, from_everyone(): lax.all_to_all(jnp.broadcast_to(array[None], (peers, *array.shape)), axis...  5.04 us
  transfers between devices with their start and end apart: 3, of which 3 were waited for; matrix products, arithmetic and copies ran while one was open for 2% of the time, Pallas kernels for 0%

commit v1 on v0

v1 whole, which is shorter than its diff:
```python
import jax
import jax.numpy as jnp
from jax import lax
from jax.experimental import pallas as pl
from jax.experimental.pallas import tpu as pltpu
from jax.sharding import Mesh
from jax.sharding import PartitionSpec as P

MESH = pl.DeviceIdType.MESH
F32 = jnp.float32
BF16 = jnp.bfloat16

softcap = 30.0

NX = 4
NR = 8
TOK = 224
TOKP = 256
WROWS = 576
CHIP = 2 * WROWS
COLS = 384
WHALF = WROWS // 2
PROWS = TOK // 2
SUBS = CHIP // COLS
GROUPS = PROWS // 16
NT = (((1,), (1,)), ((), ()))


def kernel(
    h_ref, w_ref, t_ref, tw_ref,
    loss_ref, hg_ref, wg_ref,
    hv, ht, wf, acc, a1, a2, rows, tcol, wcol, s128, t128, st1, st2, gk,
    sp, rp, sm, rm, fb, r2, og,
    ds_, dr, xs, xr, wout,
    in_sem, out_sem, w_s, w_r, st_s, st_r, p_s, p_r, m_s, m_r, f_s, f_r, g_s, g_r,
    ap_s, ap_r, am_s, am_r, d_s, d_r, x_s, x_r,
):
    x, c = lax.axis_index("x"), lax.axis_index("c")
    y, z = lax.axis_index("y"), lax.axis_index("z")
    xl, xr_, x2 = (x + NX - 1) % NX, (x + 1) % NX, (x + 2) % NX
    oc = 1 - c
    i = y * oc + z * c
    j = z * oc + y * c

    def first(n):
        return (x, c, n * oc + y * c, z * oc + n * c)

    def second(n):
        return (x, c, y * oc + n * c, n * oc + z * c)

    right, left, partner = (xr_, c, y, z), (xl, c, y, z), (x, oc, y, z)
    sent = []

    def copy(src, dst, s, r, dev):
        return pltpu.make_async_remote_copy(
            src_ref=src, dst_ref=dst, send_sem=s, recv_sem=r, device_id=dev, device_id_type=MESH
        )

    def send(src, dst, s, r, dev):
        rc = copy(src, dst, s, r, dev)
        rc.start()
        sent.append(rc)

    def arrived(dst, s, r):
        copy(dst, dst, s, r, partner).wait_recv()

    def wpart(xx, cc, h):
        return wf.at[xx, pl.ds(pl.multiple_of(cc * WROWS + h * WHALF, 32), WHALF)]

    own_rows = pl.ds(pl.multiple_of(c * WROWS, 32), WROWS)
    other_rows = pl.ds(pl.multiple_of(oc * WROWS, 32), WROWS)

    w_in = pltpu.make_async_copy(w_ref, wf.at[x, own_rows], in_sem.at[0])
    w_in.start()
    h_in = pltpu.make_async_copy(h_ref, hv.at[pl.ds(0, TOK)], in_sem.at[1])
    h_in.start()

    barrier = pltpu.get_barrier_semaphore()
    peers = [right, left, partner]
    for k in range(1, NR):
        peers.append(first((i + k) % NR))
        peers.append(second((j + k) % NR))
    for peer in peers:
        pl.semaphore_signal(barrier, inc=1, device_id=peer, device_id_type=MESH)
    pl.semaphore_wait(barrier, len(peers))

    w_in.wait()
    send(wpart(x, c, 0), wpart(x, c, 0), w_s.at[0], w_r.at[0], right)
    send(wpart(x, c, 1), wpart(x, c, 1), w_s.at[3], w_r.at[3], left)
    send(wpart(x, c, 1), wpart(x, c, 1), w_s.at[1], w_r.at[1], right)
    send(wpart(x, c, 0), wpart(x, c, 0), w_s.at[4], w_r.at[4], left)
    send(wf.at[x, own_rows], wf.at[x, own_rows], w_s.at[6], w_r.at[6], partner)

    rows[...] = jnp.zeros_like(rows)
    rows[0:1, 0:TOK] = t_ref[...].astype(F32)
    rows[1:2, 0:TOK] = tw_ref[...]
    tcol[...] = jnp.broadcast_to(rows[0:1, :], (128, TOKP)).T.astype(jnp.int32)
    wcol[...] = jnp.broadcast_to(rows[1:2, :], (128, TOKP)).T
    s128[pl.ds(TOK, TOKP - TOK)] = jnp.zeros((TOKP - TOK, 128), F32)
    t128[pl.ds(TOK, TOKP - TOK)] = jnp.zeros((TOKP - TOK, 128), F32)
    gk[pl.ds(TOK, TOKP - TOK)] = jnp.zeros((TOKP - TOK, COLS), BF16)
    hv[pl.ds(TOK, TOKP - TOK)] = jnp.zeros((TOKP - TOK, NX * CHIP), BF16)
    h_in.wait()

    def part_logits(xx):
        at = pl.ds(pl.multiple_of(xx * CHIP, 128), CHIP)
        return jnp.dot(hv[pl.ds(0, TOK), at], wf[xx], preferred_element_type=F32)

    arrived(wf.at[x, other_rows], w_s.at[6], w_r.at[6])
    acc[...] = part_logits(x)

    @pl.loop(0, NX)
    def _(n):
        @pl.loop(0, CHIP // 128)
        def _(b):
            at = pl.ds(pl.multiple_of(n * CHIP + b * 128, 128), 128)
            ht[n, pl.ds(pl.multiple_of(b * 128, 128), 128), :] = hv[:, at].T

    arrived(wpart(xl, c, 0), w_s.at[0], w_r.at[0])
    send(wpart(xl, c, 0), wpart(xl, c, 0), w_s.at[2], w_r.at[2], right)
    send(wpart(xl, c, 0), wpart(xl, c, 0), w_s.at[7], w_r.at[7], partner)
    arrived(wpart(xr_, c, 1), w_s.at[3], w_r.at[3])
    send(wpart(xr_, c, 1), wpart(xr_, c, 1), w_s.at[5], w_r.at[5], left)
    send(wpart(xr_, c, 1), wpart(xr_, c, 1), w_s.at[8], w_r.at[8], partner)
    arrived(wpart(xl, c, 1), w_s.at[1], w_r.at[1])
    send(wpart(xl, c, 1), wpart(xl, c, 1), w_s.at[9], w_r.at[9], partner)
    arrived(wpart(xr_, c, 0), w_s.at[4], w_r.at[4])
    send(wpart(xr_, c, 0), wpart(xr_, c, 0), w_s.at[10], w_r.at[10], partner)
    arrived(wpart(xl, oc, 0), w_s.at[7], w_r.at[7])
    arrived(wpart(xl, oc, 1), w_s.at[9], w_r.at[9])
    acc[...] += part_logits(xl)
    arrived(wpart(xr_, oc, 1), w_s.at[8], w_r.at[8])
    arrived(wpart(xr_, oc, 0), w_s.at[10], w_r.at[10])
    acc[...] += part_logits(xr_)
    arrived(wpart(x2, c, 0), w_s.at[2], w_r.at[2])
    send(wpart(x2, c, 0), wpart(x2, c, 0), w_s.at[11], w_r.at[11], partner)
    arrived(wpart(x2, c, 1), w_s.at[5], w_r.at[5])
    send(wpart(x2, c, 1), wpart(x2, c, 1), w_s.at[12], w_r.at[12], partner)
    arrived(wpart(x2, oc, 0), w_s.at[11], w_r.at[11])
    arrived(wpart(x2, oc, 1), w_s.at[12], w_r.at[12])
    acc[...] += part_logits(x2)

    first_col = (y * NR + z) * COLS
    used = COLS * NR * NR - COLS // 2

    @pl.loop(0, TOK // 16)
    def _(r):
        at = pl.ds(pl.multiple_of(r * 16, 16), 16)
        tgt, wgt = tcol[at], wcol[at]
        total, hits = jnp.zeros((16, 128), F32), jnp.zeros((16, 128), F32)
        for n in range(COLS // 128):
            lanes = pl.ds(n * 128, 128)
            ids = first_col + n * 128 + lax.broadcasted_iota(jnp.int32, (16, 128), 1)
            squash = jnp.tanh(acc[at, lanes] / softcap)
            capped = softcap * squash
            exps = jnp.where(ids < used, jnp.exp(capped), 0.0)
            hit = ids == tgt
            slope = wgt * (1.0 - squash * squash)
            a1[at, lanes] = slope * exps
            a2[at, lanes] = jnp.where(hit, slope, 0.0)
            total += exps
            hits += jnp.where(hit, capped, 0.0)
        s128[at] = total
        t128[at] = hits

    st1[i, 0:1, :] = jnp.sum(s128[...].T, axis=0, keepdims=True)
    st1[i, 1:2, :] = jnp.sum(t128[...].T, axis=0, keepdims=True)

    def share(st, mine, dev, base):
        for k in range(1, NR):
            send(st.at[mine], st.at[mine], st_s.at[base + k], st_r.at[base + k], dev((mine + k) % NR))
        for k in range(1, NR):
            arrived(st.at[(mine + NR - k) % NR], st_s.at[base + k], st_r.at[base + k])
        total = st[0]
        for k in range(1, NR):
            total += st[k]
        return total

    st2[j] = share(st1, i, first, 0)
    stats = share(st2, j, second, NR)
    sums = stats[0:1, :]
    loss_ref[...] = jnp.log(sums[:, 0:TOK]) - stats[1:2, 0:TOK]
    s128[...] = jnp.broadcast_to(1.0 / sums, (128, TOKP)).T

    @pl.loop(0, TOK // 16)
    def _(r):
        at = pl.ds(pl.multiple_of(r * 16, 16), 16)
        inv = s128[at]
        for n in range(COLS // 128):
            lanes = pl.ds(n * 128, 128)
            gk[at, lanes] = (a1[at, lanes] * inv - a2[at, lanes]).astype(BF16)

    up, down = first((i + 1) % NR), first((i + NR - 1) % NR)

    def piece(p, sub):
        g = gk[pl.ds(pl.multiple_of((p // NX) * PROWS, 16), PROWS), :]
        w = wf[p % NX, pl.ds(sub * COLS, COLS), :]
        return lax.dot_general(g, w, NT, preferred_element_type=F32)

    def hop_up(s, sub):
        val = piece((i + 4 - s) % NR, sub)
        if s > 1 or (s == 1 and sub < 2):
            arrived(rp.at[s - 1, sub], p_s.at[s - 1, sub], p_r.at[s - 1, sub])
            val += rp[s - 1, sub].astype(F32)
        sp[s, sub] = val.astype(BF16)
        send(sp.at[s, sub], rp.at[s, sub], p_s.at[s, sub], p_r.at[s, sub], up)

    def hop_down(s, sub):
        val = piece((i + 4 + s) % NR, sub)
        if s > 1 or (s == 1 and sub == 2):
            arrived(rm.at[s - 1, sub], m_s.at[s - 1, sub], m_r.at[s - 1, sub])
            val += rm[s - 1, sub].astype(F32)
        sm[s, sub] = val.astype(BF16)
        send(sm.at[s, sub], rm.at[s, sub], m_s.at[s, sub], m_r.at[s, sub], down)

    hop_up(0, 0)
    hop_down(0, 2)
    hop_up(0, 1)
    hop_down(1, 0)
    hop_down(1, 1)
    hop_up(1, 2)

    def term(xx, cc, h):
        a = ht[xx, pl.ds(pl.multiple_of(cc * WROWS + h * WHALF, 32), WHALF), :]
        return jnp.dot(a, gk[...], preferred_element_type=F32)

    def give(xx, h):
        ds_[xx, h] = term(xx, oc, h).astype(BF16)
        send(ds_.at[xx, h], dr.at[xx, h], d_s.at[xx, h], d_r.at[xx, h], partner)

    def chip_term(xx, h):
        val = term(xx, c, h)
        arrived(dr.at[xx, h], d_s.at[xx, h], d_r.at[xx, h])
        return val + dr[xx, h].astype(F32)

    def pass_on(n, val, dev):
        xs[n] = val.astype(BF16)
        send(xs.at[n], xr.at[n], x_s.at[n], x_r.at[n], dev)

    def got(n):
        arrived(xr.at[n], x_s.at[n], x_r.at[n])
        return xr[n].astype(F32)

    give(x2, 0)
    give(x2, 1)
    hop_up(1, 0)
    hop_down(1, 2)
    hop_up(1, 1)
    give(xr_, 1)
    give(xl, 0)
    pass_on(0, chip_term(x2, 0), right)
    pass_on(3, chip_term(x2, 1), left)
    for sub in (0, 2, 1):
        hop_up(2, sub)
        hop_down(2, 2 - sub)
    give(xr_, 0)
    give(xl, 1)
    pass_on(1, chip_term(xr_, 1), right)
    pass_on(4, chip_term(xl, 0), left)
    for sub in (0, 2, 1):
        hop_up(3, sub)
        hop_down(3, 2 - sub)
    give(x, 0)
    give(x, 1)

    for sub in range(SUBS):
        val = piece(i, sub)
        arrived(rp.at[3, sub], p_s.at[3, sub], p_r.at[3, sub])
        arrived(rm.at[3, sub], m_s.at[3, sub], m_r.at[3, sub])
        val += rp[3, sub].astype(F32) + rm[3, sub].astype(F32)
        fb[:, :, pl.ds(sub * COLS, COLS)] = val.astype(BF16).reshape(GROUPS, 16, COLS)

    for k in range(1, NR):
        g = (j + k) % NR

        @pl.when(g < GROUPS)
        def _():
            copy(fb.at[g], r2.at[j], f_s.at[k], f_r.at[k], second(g)).start()

    pass_on(2, chip_term(xr_, 0) + got(0), right)
    pass_on(5, chip_term(xl, 1) + got(3), left)

    @pl.when(j < GROUPS)
    def _():
        total = fb[j].astype(F32)
        for k in range(1, NR):
            arrived(r2.at[(j + NR - k) % NR], f_s.at[k], f_r.at[k])
            total += r2[(j + NR - k) % NR].astype(F32)
        og[i, j] = total.astype(BF16)
        for k in range(1, NR):
            copy(og.at[i, j], og.at[i, j], g_s.at[k], g_r.at[j], second((j + k) % NR)).start()

    def ring(s, g, p_up, p_down, ups, downs):
        if ups:
            send(og.at[p_up, g], og.at[p_up, g], ap_s.at[s, g], ap_r.at[s, g], up)
        if downs:
            send(og.at[p_down, g], og.at[p_down, g], am_s.at[s, g], am_r.at[s, g], down)

    for g in range(GROUPS):
        @pl.when(j != g)
        def _():
            arrived(og.at[i, g], g_s.at[0], g_r.at[g])
        ring(0, g, i, i, True, True)

    for s in range(1, 4):
        p_up, p_down = (i + NR - s) % NR, (i + s) % NR
        for g in range(GROUPS):
            arrived(og.at[p_up, g], ap_s.at[s - 1, g], ap_r.at[s - 1, g])
            arrived(og.at[p_down, g], am_s.at[s - 1, g], am_r.at[s - 1, g])
            ring(s, g, p_up, p_down, s < 3 or g < 4, s < 3 or g >= 4)

    wout[pl.ds(0, WHALF)] = (chip_term(x, 0) + got(2) + got(4)).astype(BF16)
    wout[pl.ds(WHALF, WHALF)] = (chip_term(x, 1) + got(5) + got(1)).astype(BF16)
    w_out = pltpu.make_async_copy(wout, wg_ref, out_sem.at[NR])
    w_out.start()

    far = (i + 4) % NR
    for g in range(GROUPS):
        if g < 4:
            arrived(og.at[far, g], ap_s.at[3, g], ap_r.at[3, g])
        else:
            arrived(og.at[far, g], am_s.at[3, g], am_r.at[3, g])

    outs = []
    for p in range(NR):
        for g in range(GROUPS):
            dst = hg_ref.at[pl.ds((p // NX) * PROWS + g * 16, 16), pl.ds((p % NX) * CHIP, CHIP)]
            outs.append(pltpu.make_async_copy(og.at[p, g], dst, out_sem.at[p * GROUPS + g + NR + 1]))
            outs[-1].start()
    w_out.wait()
    for o in outs:
        o.wait()

    for rc in sent:
        rc.wait_send()
    for k in range(1, NR):
        g = (j + k) % NR

        @pl.when(g < GROUPS)
        def _():
            copy(fb.at[g], r2.at[j], f_s.at[k], f_r.at[k], second(g)).wait_send()

        @pl.when(j < GROUPS)
        def _():
            copy(og.at[i, j], og.at[i, j], g_s.at[k], g_r.at[j], second(g)).wait_send()


def body(hidden, out_weight, targets, token_weight):
    dma = pltpu.SemaphoreType.DMA
    vm = pltpu.VMEM
    loss, hg, wg = pl.pallas_call(
        kernel,
        name="fused_xent",
        out_shape=(
            jax.ShapeDtypeStruct((1, TOK), F32),
            jax.ShapeDtypeStruct((TOK, NX * CHIP), BF16),
            jax.ShapeDtypeStruct((WROWS, COLS), BF16),
        ),
        in_specs=[
            pl.BlockSpec(memory_space=pl.ANY),
            pl.BlockSpec(memory_space=pl.ANY),
            pl.BlockSpec(memory_space=vm),
            pl.BlockSpec(memory_space=vm),
        ],
        out_specs=(
            pl.BlockSpec(memory_space=vm),
            pl.BlockSpec(memory_space=pl.ANY),
            pl.BlockSpec(memory_space=pl.ANY),
        ),
        scratch_shapes=[
            vm((TOKP, NX * CHIP), BF16),
            vm((NX, CHIP, TOKP), BF16),
            vm((NX, CHIP, COLS), BF16),
            vm((TOK, COLS), F32),
            vm((TOK, COLS), F32),
            vm((TOK, COLS), F32),
            vm((8, TOKP), F32),
            vm((TOKP, 128), jnp.int32),
            vm((TOKP, 128), F32),
            vm((TOKP, 128), F32),
            vm((TOKP, 128), F32),
            vm((NR, 2, TOKP), F32),
            vm((NR, 2, TOKP), F32),
            vm((TOKP, COLS), BF16),
            vm((4, SUBS, PROWS, COLS), BF16),
            vm((4, SUBS, PROWS, COLS), BF16),
            vm((4, SUBS, PROWS, COLS), BF16),
            vm((4, SUBS, PROWS, COLS), BF16),
            vm((GROUPS, 16, CHIP), BF16),
            vm((NR, 16, CHIP), BF16),
            vm((NR, GROUPS, 16, CHIP), BF16),
            vm((NX, 2, WHALF, COLS), BF16),
            vm((NX, 2, WHALF, COLS), BF16),
            vm((6, WHALF, COLS), BF16),
            vm((6, WHALF, COLS), BF16),
            vm((WROWS, COLS), BF16),
            dma((2,)), dma((NR + 1 + NR * GROUPS,)),
            dma((13,)), dma((13,)),
            dma((2 * NR,)), dma((2 * NR,)),
            dma((4, SUBS)), dma((4, SUBS)),
            dma((4, SUBS)), dma((4, SUBS)),
            dma((NR,)), dma((NR,)),
            dma((NR,)), dma((GROUPS,)),
            dma((4, GROUPS)), dma((4, GROUPS)),
            dma((4, GROUPS)), dma((4, GROUPS)),
            dma((NX, 2)), dma((NX, 2)),
            dma((6,)), dma((6,)),
        ],
        compiler_params=pltpu.CompilerParams(
            collective_id=0, has_side_effects=True, vmem_limit_bytes=60 * 1024 * 1024
        ),
    )(hidden, out_weight, targets.reshape(1, TOK), token_weight.reshape(1, TOK))
    return loss.reshape(TOK), hg, wg


def solution(mesh):
    torus = Mesh(mesh.devices.reshape(NX, 2, NR, NR), ("x", "c", "y", "z"))
    dp, vocab = ("x", "c"), ("y", "z")
    in_specs = (P(dp, None), P(dp, vocab), P(dp), P(dp))
    out_specs = (P(dp), P(dp, None), P(dp, vocab))
    return jax.shard_map(body, mesh=torus, in_specs=in_specs, out_specs=out_specs, check_vma=False)
```

time: 244 us -> 99.9 us (0.41)
  the two profiles are of different devices: /device:TPU:1 before, /device:TPU:24 now
where the time goes in v1:
time: 99.9 us; the launch traced here: 99.7 us
  Pallas kernels  94 us (94%)
  local copies, waits for them, and re-layouts  5.02 us (5%)
    pallas_call x1, Pallas kernels, body(): pl.pallas_call(kernel, name='fused_xent', out_shape=(jax.ShapeDtypeStruct...  94 us
    unnamed x5, local copies, waits for them, and re-layouts  5.02 us

profile of v1, /device:TPU:24, one launch (start us, length us, event | category | flops | bytes accessed | tf_op | source)
XLA Modules:
  0.0 99.7 jit_solution(14931923036374466586)
XLA Ops:
  0.6 94.0 %fused_xent.1 = (f32[1,224]{1,0:T(1,128)}, bf16[224,4608]{1,0:T(8,128)(2,1)}, bf16[576,384]{1,0:T(8,128)(2,1)}) custom-call(bf16[224,4608]{1,0:T(8,128)(2,1)} %h_ref.1, bf16[576,384]{1,0:T(8,128)(2,1)} %w_ref.1, s32[1,224]{1,0:T(1,128)} %bitcast.3, f32[1,224]{1,0:T(1,128)} %bitcast.4), custom_call_target="tpu_custom_call" | custom-call | tf_op jit(solution)/shard_map/fused_xent/pallas_call | solution.py:351
  94.6 1.2 %copy.10 = f32[224]{0:T(256)} copy(f32[224]{0:T(256)} %bitcast.5) | data formatting | bytes 1792
  95.8 0.0 copy-start
  95.8 3.1 %copy.11 = bf16[224,4608]{1,0:T(8,128)(2,1)} copy(bf16[224,4608]{1,0:T(8,128)(2,1)} %get-tuple-element.13) | data formatting | bytes 4128768
  98.9 0.0 copy-done
  98.9 0.8 copy.12
Async XLA Ops:
  95.8 3.1 %copy-start = (bf16[576,384]{1,0:T(8,128)(2,1)S(1)}, bf16[576,384]{1,0:T(8,128)(2,1)}, u32[]{:S(2)}) copy-start(bf16[576,384]{1,0:T(8,128)(2,1)} %get-tuple-element.14) | copy-start | bytes 1327108

commit v2 on v1

v2 whole, which is shorter than its diff:
```python
import jax
import jax.numpy as jnp
from jax import lax
from jax.experimental import pallas as pl
from jax.experimental.pallas import tpu as pltpu
from jax.sharding import Mesh
from jax.sharding import PartitionSpec as P

MESH = pl.DeviceIdType.MESH
F32 = jnp.float32
BF16 = jnp.bfloat16

softcap = 30.0

NX = 4
NR = 8
TOK = 224
TOKP = 256
WROWS = 576
CHIP = 2 * WROWS
COLS = 384
WHALF = WROWS // 2
PROWS = TOK // 2
SUBS = CHIP // COLS
GROUPS = PROWS // 16
NT = (((1,), (1,)), ((), ()))
FAR_FIRST = (4, 3, 5, 2, 6, 1, 7, 0)
NEAR_FIRST = (0, 1, 7, 2, 6, 3, 5, 4)
UP4 = (4, 5, 6, 7)


def kernel(
    h_ref, w_ref, t_ref, tw_ref,
    loss_ref, og, wout,
    hv, ht, wf, acc, a1, a2, ab, pu, tin, win, rows, tcol, wcol, s128, t128, st1, st2, gk,
    sp, rp, sm, rm, fb, r2, ds_, dr, xs, xr,
    in_sem, w_s, w_r, st_s, st_r, p_s, p_r, m_s, m_r, f_s, f_r, g_s, g_r,
    ap_s, ap_r, am_s, am_r, d_s, d_r, x_s, x_r,
):
    x, c = lax.axis_index("x"), lax.axis_index("c")
    y, z = lax.axis_index("y"), lax.axis_index("z")
    xl, xr_, x2 = (x + NX - 1) % NX, (x + 1) % NX, (x + 2) % NX
    oc = 1 - c
    i = y * oc + z * c
    j = z * oc + y * c

    def first(n):
        return (x, c, n * oc + y * c, z * oc + n * c)

    def second(n):
        return (x, c, y * oc + n * c, n * oc + z * c)

    right, left, partner = (xr_, c, y, z), (xl, c, y, z), (x, oc, y, z)
    up, down = first((i + 1) % NR), first((i + NR - 1) % NR)

    def copy(src, dst, s, r, dev):
        return pltpu.make_async_remote_copy(
            src_ref=src, dst_ref=dst, send_sem=s, recv_sem=r, device_id=dev, device_id_type=MESH
        )

    def send(src, dst, s, r, dev):
        copy(src, dst, s, r, dev).start()

    def arrived(dst, s, r):
        copy(dst, dst, s, r, partner).wait_recv()

    def all_sent(refs, s, r):
        copy(refs, refs, s, r, partner).wait_send()

    own_rows = pl.ds(pl.multiple_of(c * WROWS, 32), WROWS)
    other_rows = pl.ds(pl.multiple_of(oc * WROWS, 32), WROWS)
    w_in = pltpu.make_async_copy(w_ref, wf.at[x, own_rows], in_sem.at[0])
    w_in.start()
    h_in = pltpu.make_async_copy(h_ref, hv.at[pl.ds(0, TOK)], in_sem.at[1])
    h_in.start()
    t_in = pltpu.make_async_copy(t_ref, tin, in_sem.at[2])
    t_in.start()
    tw_in = pltpu.make_async_copy(tw_ref, win, in_sem.at[3])
    tw_in.start()

    barrier = pltpu.get_barrier_semaphore()
    peers = [right, left, partner]
    for k in range(1, NR):
        peers.append(first((i + k) % NR))
        peers.append(second((j + k) % NR))
    for peer in peers:
        pl.semaphore_signal(barrier, inc=1, device_id=peer, device_id_type=MESH)
    pl.semaphore_wait(barrier, len(peers))

    def wpart(xx, cc, h):
        return wf.at[xx, pl.ds(pl.multiple_of(cc * WROWS + h * WHALF, 32), WHALF)]

    def wsend(xx, h, n, dev):
        send(wpart(xx, c, h), wpart(xx, c, h), w_s.at[0], w_r.at[n], dev)

    def wgot(xx, cc, h, n):
        arrived(wpart(xx, cc, h), w_s.at[0], w_r.at[n])

    w_in.wait()
    wsend(x, 0, 0, right)
    wsend(x, 1, 3, left)
    wsend(x, 1, 1, right)
    wsend(x, 0, 4, left)
    send(wf.at[x, own_rows], wf.at[x, own_rows], w_s.at[0], w_r.at[6], partner)

    t_in.wait()
    tw_in.wait()
    rows[...] = jnp.zeros_like(rows)
    rows[0:1, 0:TOK] = tin[...].astype(F32)
    rows[1:2, 0:TOK] = win[...]
    tcol[...] = jnp.broadcast_to(rows[0:1, :], (128, TOKP)).T.astype(jnp.int32)
    wcol[...] = jnp.broadcast_to(rows[1:2, :], (128, TOKP)).T
    pad = pl.ds(TOK, TOKP - TOK)
    s128[pad] = jnp.zeros((TOKP - TOK, 128), F32)
    t128[pad] = jnp.zeros((TOKP - TOK, 128), F32)
    gk[pad] = jnp.zeros((TOKP - TOK, COLS), BF16)
    hv[pad] = jnp.zeros((TOKP - TOK, NX * CHIP), BF16)
    h_in.wait()

    def part_logits(xx):
        at = pl.ds(pl.multiple_of(xx * CHIP, 128), CHIP)
        return jnp.dot(hv[pl.ds(0, TOK), at], wf[xx], preferred_element_type=F32)

    arrived(wf.at[x, other_rows], w_s.at[0], w_r.at[6])
    acc[...] = part_logits(x)

    @pl.loop(0, NX)
    def _(n):
        @pl.loop(0, CHIP // 128)
        def _(b):
            at = pl.ds(pl.multiple_of(n * CHIP + b * 128, 128), 128)
            ht[n, pl.ds(pl.multiple_of(b * 128, 128), 128), :] = hv[:, at].T

    wgot(xl, c, 0, 0)
    wsend(xl, 0, 2, right)
    wsend(xl, 0, 7, partner)
    wgot(xr_, c, 1, 3)
    wsend(xr_, 1, 5, left)
    wsend(xr_, 1, 8, partner)
    wgot(xl, c, 1, 1)
    wsend(xl, 1, 9, partner)
    wgot(xr_, c, 0, 4)
    wsend(xr_, 0, 10, partner)
    wgot(xl, oc, 0, 7)
    wgot(xl, oc, 1, 9)
    acc[...] += part_logits(xl)
    wgot(xr_, oc, 1, 8)
    wgot(xr_, oc, 0, 10)
    acc[...] += part_logits(xr_)
    wgot(x2, c, 0, 2)
    wsend(x2, 0, 11, partner)
    wgot(x2, c, 1, 5)
    wsend(x2, 1, 12, partner)
    wgot(x2, oc, 0, 11)
    wgot(x2, oc, 1, 12)
    acc[...] += part_logits(x2)

    first_col = (y * NR + z) * COLS
    used = COLS * NR * NR - COLS // 2

    @pl.loop(0, TOK // 16)
    def _(r):
        at = pl.ds(pl.multiple_of(r * 16, 16), 16)
        at2 = pl.ds(pl.multiple_of(TOK + r * 16, 16), 16)
        tgt, wgt = tcol[at], wcol[at]
        total, hits = jnp.zeros((16, 128), F32), jnp.zeros((16, 128), F32)
        for n in range(COLS // 128):
            lanes = pl.ds(n * 128, 128)
            ids = first_col + n * 128 + lax.broadcasted_iota(jnp.int32, (16, 128), 1)
            squash = jnp.tanh(acc[at, lanes] / softcap)
            capped = softcap * squash
            exps = jnp.where(ids < used, jnp.exp(capped), 0.0)
            hit = ids == tgt
            slope = wgt * (1.0 - squash * squash)
            grown, single = slope * exps, jnp.where(hit, slope, 0.0)
            a1[at, lanes] = grown
            a2[at, lanes] = single
            ab[at, lanes] = grown.astype(BF16)
            ab[at2, lanes] = single.astype(BF16)
            total += exps
            hits += jnp.where(hit, capped, 0.0)
        s128[at] = total
        t128[at] = hits

    st1[i, 0:1, :] = jnp.sum(s128[...].T, axis=0, keepdims=True)
    st1[i, 1:2, :] = jnp.sum(t128[...].T, axis=0, keepdims=True)

    def share(st, mine, dev, n):
        for k in FAR_FIRST[:-1]:
            send(st.at[mine], st.at[mine], st_s.at[n], st_r.at[n, k], dev((mine + k) % NR))

    def shared(st, mine, n):
        for k in NEAR_FIRST[1:]:
            arrived(st.at[(mine + NR - k) % NR], st_s.at[n], st_r.at[n, k])
        total = st[0]
        for k in range(1, NR):
            total += st[k]
        return total

    def products(lo):
        @pl.loop(0, 2 * SUBS)
        def _(n):
            b, at = lo + n // SUBS, pl.ds(pl.multiple_of((n % SUBS) * COLS, 128), COLS)
            pu[b, :, at] = lax.dot_general(ab[...], wf[b, at, :], NT, preferred_element_type=F32)

    share(st1, i, first, 0)
    products(0)
    st2[j] = shared(st1, i, 0)
    share(st2, j, second, 1)
    products(2)
    stats = shared(st2, j, 1)
    sums = stats[0:1, :]
    loss_ref[...] = jnp.log(sums[:, 0:TOK]) - stats[1:2, 0:TOK]
    s128[...] = jnp.broadcast_to(1.0 / sums, (128, TOKP)).T

    def chunk(p, g):
        row = (p // NX) * PROWS + g * 16
        at, at2 = pl.ds(pl.multiple_of(row, 16), 16), pl.ds(pl.multiple_of(TOK + row, 16), 16)
        inv = jnp.concatenate([s128[at]] * (CHIP // 128), axis=1)
        return pu[p % NX, at, :] * inv - pu[p % NX, at2, :]

    def hop(s, o, p, out, into, s_sem, r_sem, dev, adds):
        g = (j + o) % NR

        @pl.when(g < GROUPS)
        def _():
            val = chunk(p, g)
            if adds:
                arrived(into.at[s - 1, o], s_sem.at[0], r_sem.at[s - 1, o])
                val += into[s - 1, o].astype(F32)
            out[s, o] = val.astype(BF16)
            send(out.at[s, o], into.at[s, o], s_sem.at[min(s, 1)], r_sem.at[s, o], dev)

    def hop_up(s, o):
        hop(s, o, (i + 4 - s) % NR, sp, rp, p_s, p_r, up, s > 1 or (s == 1 and o in UP4))

    def hop_down(s, o):
        hop(s, o, (i + 4 + s) % NR, sm, rm, m_s, m_r, down, s > 1 or (s == 1 and o not in UP4))

    for o in FAR_FIRST:
        (hop_up if o in UP4 else hop_down)(0, o)
    for o in FAR_FIRST:
        (hop_down if o in UP4 else hop_up)(1, o)

    @pl.loop(0, TOK // 16)
    def _(r):
        at = pl.ds(pl.multiple_of(r * 16, 16), 16)
        inv = s128[at]
        for n in range(COLS // 128):
            lanes = pl.ds(n * 128, 128)
            gk[at, lanes] = (a1[at, lanes] * inv - a2[at, lanes]).astype(BF16)

    def term(xx, cc, h):
        a = ht[xx, pl.ds(pl.multiple_of(cc * WROWS + h * WHALF, 32), WHALF), :]
        return jnp.dot(a, gk[...], preferred_element_type=F32)

    def give(xx, h):
        ds_[xx, h] = term(xx, oc, h).astype(BF16)
        send(ds_.at[xx, h], dr.at[xx, h], d_s.at[0], d_r.at[xx, h], partner)

    def chip_term(xx, h):
        val = term(xx, c, h)
        arrived(dr.at[xx, h], d_s.at[0], d_r.at[xx, h])
        return val + dr[xx, h].astype(F32)

    def pass_on(n, val, dev):
        xs[n] = val.astype(BF16)
        send(xs.at[n], xr.at[n], x_s.at[0], x_r.at[n], dev)

    def got(n):
        arrived(xr.at[n], x_s.at[0], x_r.at[n])
        return xr[n].astype(F32)

    give(x2, 0)
    give(x2, 1)
    for o in FAR_FIRST:
        (hop_up if o in UP4 else hop_down)(1, o)
    give(xr_, 1)
    give(xl, 0)
    for o in FAR_FIRST:
        hop_up(2, o)
        hop_down(2, o)
    pass_on(0, chip_term(x2, 0), right)
    pass_on(3, chip_term(x2, 1), left)
    for o in FAR_FIRST:
        hop_up(3, o)
        hop_down(3, o)
    pass_on(1, chip_term(xr_, 1), right)
    pass_on(4, chip_term(xl, 0), left)

    for o in FAR_FIRST:
        g = (j + o) % NR

        @pl.when(g < GROUPS)
        def _():
            val = chunk(i, g)
            arrived(rp.at[3, o], p_s.at[0], p_r.at[3, o])
            arrived(rm.at[3, o], m_s.at[0], m_r.at[3, o])
            val += rp[3, o].astype(F32) + rm[3, o].astype(F32)
            fb[o] = val.astype(BF16)
            if o:
                send(fb.at[o], r2.at[o], f_s.at[0], f_r.at[o], second(g))

    give(xr_, 0)
    give(xl, 1)
    give(x, 0)
    give(x, 1)

    def og_at(p, g):
        return og.at[p, pl.ds(pl.multiple_of(g * 16, 16), 16)]

    @pl.when(j < GROUPS)
    def _():
        total = fb[0].astype(F32)
        for o in NEAR_FIRST[1:]:
            arrived(r2.at[o], f_s.at[0], f_r.at[o])
            total += r2[o].astype(F32)
        og[i, pl.ds(pl.multiple_of(j * 16, 16), 16)] = total.astype(BF16)
        for k in FAR_FIRST[:-1]:
            send(og_at(i, j), og_at(i, j), g_s.at[0], g_r.at[NR - k], second((j + k) % NR))

    def ring(s, o, g, p_up, p_down):
        if s < 3 or o in UP4:
            send(og_at(p_up, g), og_at(p_up, g), ap_s.at[s // 3], ap_r.at[s, o], up)
        if s < 3 or o not in UP4:
            send(og_at(p_down, g), og_at(p_down, g), am_s.at[s // 3], am_r.at[s, o], down)

    for o in NEAR_FIRST:
        g = (j + o) % NR

        @pl.when(g < GROUPS)
        def _():
            if o:
                arrived(og_at(i, g), g_s.at[0], g_r.at[o])
            ring(0, o, g, i, i)

    pass_on(2, chip_term(xr_, 0) + got(0), right)
    pass_on(5, chip_term(xl, 1) + got(3), left)

    for s in range(1, 4):
        p_up, p_down = (i + NR - s) % NR, (i + s) % NR
        for o in NEAR_FIRST:
            g = (j + o) % NR

            @pl.when(g < GROUPS)
            def _():
                arrived(og_at(p_up, g), ap_s.at[0], ap_r.at[s - 1, o])
                arrived(og_at(p_down, g), am_s.at[0], am_r.at[s - 1, o])
                ring(s, o, g, p_up, p_down)

    wout[pl.ds(0, WHALF)] = (chip_term(x, 0) + got(2) + got(4)).astype(BF16)
    wout[pl.ds(WHALF, WHALF)] = (chip_term(x, 1) + got(5) + got(1)).astype(BF16)

    far = (i + 4) % NR
    for o in NEAR_FIRST:
        g = (j + o) % NR

        @pl.when(g < GROUPS)
        def _():
            if o in UP4:
                arrived(og_at(far, g), ap_s.at[0], ap_r.at[3, o])
            else:
                arrived(og_at(far, g), am_s.at[0], am_r.at[3, o])

    all_sent(wf.at[:, pl.ds(0, 14 * WHALF // NX)], w_s.at[0], w_r.at[0])
    all_sent(st1.at[pl.ds(0, NR - 1)], st_s.at[0], st_r.at[0, 0])
    all_sent(st2.at[pl.ds(0, NR - 1)], st_s.at[1], st_r.at[1, 0])
    all_sent(ds_, d_s.at[0], d_r.at[0, 0])
    all_sent(xs, x_s.at[0], x_r.at[0])
    for ring_s, ring_r in ((p_s, p_r), (m_s, m_r)):
        all_sent(sp.at[pl.ds(0, 3), pl.ds(0, GROUPS)], ring_s.at[1], ring_r.at[0, 0])
    for ring_s, ring_r in ((ap_s, ap_r), (am_s, am_r)):
        all_sent(sp.at[pl.ds(0, 3), pl.ds(0, GROUPS)], ring_s.at[0], ring_r.at[0, 0])

    def fourth(n_up, n_down):
        all_sent(sp.at[0, pl.ds(0, n_up)], p_s.at[0], p_r.at[0, 0])
        all_sent(sp.at[0, pl.ds(0, n_down)], m_s.at[0], m_r.at[0, 0])
        all_sent(sp.at[0, pl.ds(0, n_up)], ap_s.at[1], ap_r.at[0, 0])
        all_sent(sp.at[0, pl.ds(0, n_down)], am_s.at[1], am_r.at[0, 0])

    @pl.when(j < 4)
    def _():
        fourth(3, 4)

    @pl.when(j >= 4)
    def _():
        fourth(4, 3)

    @pl.when(j < GROUPS)
    def _():
        all_sent(fb.at[pl.ds(0, NR - 2)], f_s.at[0], f_r.at[0])
        all_sent(fb.at[pl.ds(0, NR - 1)], g_s.at[0], g_r.at[0])

    @pl.when(j >= GROUPS)
    def _():
        all_sent(fb.at[pl.ds(0, NR - 1)], f_s.at[0], f_r.at[0])


def finish(loss_in, og, w_in, loss_ref, hg_ref, wg_ref, sem):
    copies = [
        pltpu.make_async_copy(
            og.at[p], hg_ref.at[pl.ds((p // NX) * PROWS, PROWS), pl.ds((p % NX) * CHIP, CHIP)], sem.at[p]
        )
        for p in range(NR)
    ]
    copies.append(pltpu.make_async_copy(w_in, wg_ref, sem.at[NR]))
    copies.append(pltpu.make_async_copy(loss_in, loss_ref, sem.at[NR + 1]))
    for one in copies:
        one.start()
    for one in copies:
        one.wait()


def body(hidden, out_weight, targets, token_weight):
    dma = pltpu.SemaphoreType.DMA
    vm = pltpu.VMEM
    anywhere, inside = pl.BlockSpec(memory_space=pl.ANY), pl.BlockSpec(memory_space=vm)
    chunks = vm((4, NR, 16, CHIP), BF16)
    loss, og, wout = pl.pallas_call(
        kernel,
        name="fused_xent",
        out_shape=(
            vm((1, TOK), F32),
            vm((NR, PROWS, CHIP), BF16),
            vm((WROWS, COLS), BF16),
        ),
        in_specs=[anywhere] * 4,
        out_specs=(inside,) * 3,
        scratch_shapes=[
            vm((TOKP, NX * CHIP), BF16),
            vm((NX, CHIP, TOKP), BF16),
            vm((NX, CHIP, COLS), BF16),
            vm((TOK, COLS), F32),
            vm((TOK, COLS), F32),
            vm((TOK, COLS), F32),
            vm((2 * TOK, COLS), BF16),
            vm((NX, 2 * TOK, CHIP), F32),
            vm((1, TOK), jnp.int32),
            vm((1, TOK), F32),
            vm((8, TOKP), F32),
            vm((TOKP, 128), jnp.int32),
            vm((TOKP, 128), F32),
            vm((TOKP, 128), F32),
            vm((TOKP, 128), F32),
            vm((NR, 2, TOKP), F32),
            vm((NR, 2, TOKP), F32),
            vm((TOKP, COLS), BF16),
            chunks, chunks, chunks, chunks,
            vm((NR, 16, CHIP), BF16),
            vm((NR, 16, CHIP), BF16),
            vm((NX, 2, WHALF, COLS), BF16),
            vm((NX, 2, WHALF, COLS), BF16),
            vm((6, WHALF, COLS), BF16),
            vm((6, WHALF, COLS), BF16),
            dma((4,)),
            dma((1,)), dma((13,)),
            dma((2,)), dma((2, NR)),
            dma((2,)), dma((4, NR)),
            dma((2,)), dma((4, NR)),
            dma((1,)), dma((NR,)),
            dma((1,)), dma((NR,)),
            dma((2,)), dma((4, NR)),
            dma((2,)), dma((4, NR)),
            dma((1,)), dma((NX, 2)),
            dma((1,)), dma((6,)),
        ],
        compiler_params=pltpu.CompilerParams(
            collective_id=0, has_side_effects=True, vmem_limit_bytes=48 * 1024 * 1024
        ),
    )(*[
        pltpu.with_memory_space_constraint(one, pltpu.HBM)
        for one in (hidden, out_weight, targets.reshape(1, TOK), token_weight.reshape(1, TOK))
    ])
    loss, hg, wg = pl.pallas_call(
        finish,
        name="to_hbm",
        out_shape=(
            jax.ShapeDtypeStruct((1, TOK), F32),
            jax.ShapeDtypeStruct((TOK, NX * CHIP), BF16),
            jax.ShapeDtypeStruct((WROWS, COLS), BF16),
        ),
        in_specs=[inside] * 3,
        out_specs=(anywhere,) * 3,
        scratch_shapes=[dma((NR + 2,))],
    )(*[pltpu.with_memory_space_constraint(one, pltpu.VMEM) for one in (loss, og, wout)])
    return loss.reshape(TOK), hg, wg


def solution(mesh):
    torus = Mesh(mesh.devices.reshape(NX, 2, NR, NR), ("x", "c", "y", "z"))
    dp, vocab = ("x", "c"), ("y", "z")
    in_specs = (P(dp, None), P(dp, vocab), P(dp), P(dp))
    out_specs = (P(dp), P(dp, None), P(dp, vocab))
    return jax.shard_map(body, mesh=torus, in_specs=in_specs, out_specs=out_specs, check_vma=False)
```

time: 99.9 us -> 88 us (0.88)
  the two profiles are of different devices: /device:TPU:24 before, /device:TPU:2 now
where the time goes in v2:
time: 88 us; the launch traced here: 87.9 us
  Pallas kernels  87.3 us (99%)
    pallas_call x1, Pallas kernels, body(): pl.pallas_call(kernel, name='fused_xent', out_shape=(vm((1, TOK), F32), v...  85.7 us

profile of v2, /device:TPU:2, one launch (start us, length us, event | category | flops | bytes accessed | tf_op | source)
XLA Modules:
  0.0 87.9 jit_solution(5939281357471146330)
XLA Ops:
  0.6 85.7 %fused_xent.1 = (f32[1,224]{1,0:T(1,128)S(1)}, bf16[8,112,1152]{2,1,0:T(8,128)(2,1)S(1)}, bf16[576,384]{1,0:T(8,128)(2,1)S(1)}) custom-call(bf16[224,4608]{1,0:T(8,128)(2,1)} %h_ref.1, bf16[576,384]{1,0:T(8,128)(2,1)} %w_ref.1, s32[1,224]{1,0:T(1,128)} %bitcast.3, f32[1,224]{1,0:T(1,128)} %bitcast.4), custom_call_target="tpu_custom_call" | custom-call | tf_op jit(solution)/shard_map/fused_xent/pallas_call | solution.py:419
  86.4 1.5 %to_hbm.1 = (f32[1,224]{1,0:T(1,128)}, bf16[224,4608]{1,0:T(8,128)(2,1)}, bf16[576,384]{1,0:T(8,128)(2,1)}) custom-call(f32[1,224]{1,0:T(1,128)S(1)} %get-tuple-element.9.loss_in, bf16[8,112,1152]{2,1,0:T(8,128)(2,1)S(1)} %get-tuple-element.10.og, bf16[576,384]{1,0:T(8,128)(2,1)S(1)} %get-tuple-element.11.w_in), custom_call_target="tpu_custom_call" | custom-call | tf_op jit(solution)/shard_map/to_hbm/pallas_call | solution.py:474
